TPU v7x, 32 devices: a whole 2x2x4 slice. The times are simulated.
32 devices in a mesh: slab: 32 (over z, y, x, core).
Axes of the slice: x: 2, y: 2, z: 4, core: 2. Of those that a mesh axis runs over, the one named last changes fastest.
Arguments:
- points: float32 [4, 128, 128, 64], P(None, 'slab'), may hold values from -6 to 6
- offsets_x: int32 [256], replicated, may hold values from 0 to 124, as said below
- coeffs_x: float32 [4, 256], replicated, may hold values from 0.1 to 1
- offsets_y: int32 [256], replicated, may hold values from 0 to 124, as said below
- coeffs_y: float32 [4, 256], replicated, may hold values from 0.1 to 1
- offsets_z: int32 [128], replicated, may hold values from 0 to 60, as said below
- coeffs_z: float32 [4, 128], replicated, may hold values from 0.1 to 1
Outputs:
- refined: float32 [4, 256, 256, 128], P(None, None, 'slab')
Inputs may be any that keep to these rules, and one draw needn't show every extreme that they name: offsets_x[i] lies between i // 2 - 2 and i // 2, clipped to 0 .. 124. offsets_y[i] lies between i // 2 - 2 and i // 2, clipped to 0 .. 124. offsets_z[i] lies between i // 2 - 2 and i // 2, clipped to 0 .. 60.
All inputs are finite; a program needn't handle non-finite values.
Results may differ from a plain program's by a relative error of at most 0.000073.
Values sent between devices are 32-bit elements; how exact they have to be, the bound alone decides.
A program may use at most 64 MiB of HBM per device.

v0:
```python
import jax
import jax.numpy as jnp
from jax import lax
from jax.sharding import PartitionSpec as P


def band_matrix(offsets, coeffs, width, start):
    weights = coeffs / jnp.sum(coeffs, axis=0, keepdims=True)
    columns = jnp.arange(width, dtype=jnp.int32)[None, :]
    first = (offsets - start)[:, None]
    matrix = jnp.zeros((offsets.shape[0], width), jnp.float32)
    for k in range(4):
        matrix = matrix + jnp.where(columns == first + k, weights[k][:, None], 0.0)
    return matrix


def along_x(matrix, grid):
    return jnp.einsum("ia,cayz->ciyz", matrix, grid, precision=lax.Precision.HIGHEST)


def along_y(matrix, grid):
    return jnp.einsum("jb,cibz->cijz", matrix, grid, precision=lax.Precision.HIGHEST)


def along_z(matrix, grid):
    return jnp.einsum("le,cije->cijl", matrix, grid, precision=lax.Precision.HIGHEST)


def body(points, offsets_x, coeffs_x, offsets_y, coeffs_y, offsets_z, coeffs_z):
    coarse_y = points.shape[2]
    coarse_z = points.shape[3]
    matrix_y = band_matrix(offsets_y, coeffs_y, coarse_y, 0)
    matrix_z = band_matrix(offsets_z, coeffs_z, coarse_z, 0)
    grid = along_y(matrix_y, points)
    grid = lax.all_to_all(grid, "slab", split_axis=2, concat_axis=1, tiled=True)
    matrix_x = band_matrix(offsets_x, coeffs_x, grid.shape[1], 0)
    grid = along_x(matrix_x, grid)
    return along_z(matrix_z, grid)


def solution(mesh):
    return jax.shard_map(
        body,
        mesh=mesh,
        in_specs=(P(None, "slab", None, None), P(), P(), P(), P(), P(), P()),
        out_specs=P(None, None, "slab", None),
        check_vma=False,
    )
```

profile of v0, /device:TPU:0, one launch (start us, length us, event | category | flops | bytes accessed | tf_op | source)
XLA Modules:
  0.0 67.6 jit_solution(16214703891033774522)
XLA Ops:
  0.0 0.0 copy-start
  0.0 0.8 %reduce_sum.27 = f32[256]{0:T(256)S(1)} reduce(f32[4,256]{1,0:T(4,128)} %param.11, f32[]{:T(128)} %constant.4.clone.1), dimensions={0}, to_apply=%region_0.0 | reduce | flops 768 | bytes 5124 | tf_op jit(solution)/shard_map/reduce_sum | solution.py:8
  0.8 0.7 %broadcast_divide_fusion.1 = f32[4,256]{1,0:T(4,128)S(1)} fusion(f32[4,256]{1,0:T(4,128)} %param.11, f32[256]{0:T(256)S(1)} %reduce_sum.27), kind=kLoop, calls=%fused_computation.70 | loop fusion | flops 1024 | bytes 9216 | tf_op jit(solution)/shard_map/div | solution.py:8
  1.5 0.7 %broadcast_add_fusion.5 = (s32[256]{0:T(256)S(1)}, s32[256]{0:T(256)S(1)}, s32[256]{0:T(256)S(1)}) fusion(s32[256]{0:T(256)} %param.10), kind=kLoop, calls=%fused_computation.81 | loop fusion | flops 768 | bytes 4096 | tf_op jit(solution)/shard_map/add | solution.py:13
  2.2 0.0 copy-done
  2.2 2.9 %convolution_bitcast_fusion = f32[4,4,256,64]{2,3,1,0:T(8,128)} fusion(f32[4,4,128,64]{2,3,1,0:T(8,128)S(1)} %copy-done, f32[256]{0:T(256)S(1)} %bitcast.50, s32[256]{0:T(256)S(1)} %get-tuple-element.21, f32[256]{0:T(256)S(1)} %bitcast.51, s32[256]{0:T(256)S(1)} %get-tuple-element.22, f32[256]{0:T(256)S(1)} %bitcast.52, s32[256]{0:T(256)S(1)} %get-tuple-element.20, ...), kind=kOutput, calls=%fused_computation.5 | convolution fusion | flops 403013632 | bytes 1581056 | tf_op jit(solution)/shard_map/jb,cibz->cijz/dot_general | solution.py:22
  5.1 2.3 %copy.12 = f32[4,4,256,64]{3,1,0,2:T(4,128)S(1)} copy(f32[4,4,256,64]{2,3,1,0:T(8,128)} %convolution_bitcast_fusion) | data formatting | bytes 2097152 | tf_op jit(solution)/shard_map/jb,cibz->cijz/transpose | solution.py:22
  7.4 0.0 copy-start.2
  7.4 0.0 copy-start.1
  7.4 0.0 copy-start.4
  7.4 0.0 copy-start.3
  7.4 2.9 %reshape.39 = f32[32,1,8192]{2,1,0:T(1,128)} reshape(f32[256,4,4,64]{3,2,1,0:T(4,128)S(1)} %bitcast.45) | data formatting | bytes 2097152
  10.3 7.3 %all-to-all-start = ((f32[32,1,8192]{2,1,0:T(1,128)}), f32[32,1,8192]{2,1,0:T(1,128)S(1)}, u32[]{:S(2)}, u32[]{:S(2)}) async-start(f32[32,1,8192]{2,1,0:T(1,128)} %reshape.39), calls=%async_computation | async-start | bytes 2097152 | tf_op jit(solution)/shard_map/all_to_all | solution.py:35
  17.7 0.0 copy-done.2
  17.7 0.0 copy-done.1
  17.7 0.0 copy-done.4
  17.8 0.0 copy-done.3
  17.8 26.0 %all-to-all-done = f32[32,1,8192]{2,1,0:T(1,128)S(1)} async-done(((f32[32,1,8192]{2,1,0:T(1,128)}), f32[32,1,8192]{2,1,0:T(1,128)S(1)}, u32[]{:S(2)}, u32[]{:S(2)}) %all-to-all-start) | async-done | bytes 1048608 | tf_op jit(solution)/shard_map/all_to_all | solution.py:35
  43.9 0.5 broadcast.42
  44.4 4.4 %reduce = f32[32,8192]{1,0:T(8,128)} reduce(f32[32,1,8192]{2,1,0:T(1,128)S(1)} %all-to-all-done, f32[]{:T(128)} %broadcast.42), dimensions={1}, to_apply=%all_to_all.13.reduce_sub_computation | reduce | bytes 2097156 | tf_op jit(solution)/shard_map/all_to_all | solution.py:35
  48.8 2.8 %reshape.40 = f32[256,4,4,64]{3,2,1,0:T(4,128)S(1)} reshape(f32[32,8192]{1,0:T(8,128)} %reduce) | data formatting | bytes 2097152
  51.6 0.7 %copy.23 = f32[4,4,256,64]{3,2,1,0:T(8,128)S(1)} copy(f32[4,4,256,64]{3,1,0,2:T(4,128)S(1)} %bitcast.47) | data formatting | bytes 2097152 | tf_op jit(solution)/shard_map/all_to_all | solution.py:35
  52.3 0.3 copy.14
  52.6 3.8 %fusion.2 = f32[4,8,64,256]{3,2,1,0:T(8,128)S(1)} fusion(f32[4,128,8,64]{3,2,1,0:T(8,128)S(1)} %bitcast.46, f32[256]{0:T(256)S(1)} %bitcast.54, s32[256]{0:T(256)S(1)} %get-tuple-element.18, f32[256]{0:T(256)S(1)} %bitcast.55, s32[256]{0:T(256)S(1)} %get-tuple-element.19, f32[256]{0:T(256)S(1)} %bitcast.56, s32[256]{0:T(256)S(1)} %get-tuple-element.17, ...), kind=kOutput, calls=%fused_computation.2 | convolution fusion | flops 805666816 | bytes 3153920 | tf_op jit(solution)/shard_map/ia,cayz->ciyz/dot_general | solution.py:18
  56.4 6.8 %fusion = f32[4,256,8,128]{3,1,2,0:T(8,128)S(1)} fusion(f32[4,8,64,256]{3,2,1,0:T(8,128)S(1)} %fusion.2, f32[128]{0:T(128)S(1)} %get-tuple-element.14, s32[128]{0:T(128)S(1)} %get-tuple-element.24, f32[128]{0:T(128)S(1)} %get-tuple-element.15, s32[128]{0:T(128)S(1)} %get-tuple-element.25, f32[128]{0:T(128)S(1)} %get-tuple-element.16, ...), kind=kOutput, calls=%fused_computation | convolution fusion | flops 805396480 | bytes 6295552 | tf_op jit(solution)/shard_map/le,cije->cijl/dot_general | solution.py:26
  63.1 4.4 %copy.16 = f32[4,256,8,128]{3,2,1,0:T(8,128)} copy(f32[4,256,8,128]{3,1,2,0:T(8,128)S(1)} %fusion) | data formatting | bytes 8388608 | tf_op jit(solution)/shard_map/le,cije->cijl/dot_general | solution.py:26
  (9 shorter events, 0.1 us)
Async XLA Ops:
  0.0 2.2 %copy-start = (f32[4,4,128,64]{2,3,1,0:T(8,128)S(1)}, f32[4,4,128,64]{2,3,1,0:T(8,128)}, u32[]{:S(2)}) copy-start(f32[4,4,128,64]{2,3,1,0:T(8,128)} %param.7) | copy-start | bytes 1572868
  7.4 10.3 %copy-start.2 = (f32[4,128]{1,0:T(4,128)S(1)}, f32[4,128]{1,0:T(4,128)}, u32[]{:S(2)}) copy-start(f32[4,128]{1,0:T(4,128)} %param.13) | copy-start | bytes 6148
  7.4 10.3 %copy-start.1 = (f32[4,256]{1,0:T(4,128)S(1)}, f32[4,256]{1,0:T(4,128)}, u32[]{:S(2)}) copy-start(f32[4,256]{1,0:T(4,128)} %param.9) | copy-start | bytes 12292
  7.4 10.3 %copy-start.4 = (s32[128]{0:T(128)S(1)}, s32[128]{0:T(128)}, u32[]{:S(2)}) copy-start(s32[128]{0:T(128)} %param.12) | copy-start | bytes 1540
  7.4 10.3 %copy-start.3 = (s32[256]{0:T(256)S(1)}, s32[256]{0:T(256)}, u32[]{:S(2)}) copy-start(s32[256]{0:T(256)} %param.8) | copy-start | bytes 3076
  10.3 33.5 %all-to-all-start = ((f32[32,1,8192]{2,1,0:T(1,128)}), f32[32,1,8192]{2,1,0:T(1,128)S(1)}, u32[]{:S(2)}, u32[]{:S(2)}) async-start(f32[32,1,8192]{2,1,0:T(1,128)} %reshape.39), calls=%async_computation | async-start | bytes 2097152 | tf_op jit(solution)/shard_map/all_to_all | solution.py:35
where the time goes:
time: 67.9 us; the launch traced here: 67.6 us
  waiting for transfers between devices  26 us (38%)
  local copies, waits for them, and re-layouts  14 us (21%)
  matrix products  13.5 us (20%)
  starting transfers between devices  7.32 us (11%)
  other arithmetic  6.6 us (10%)
    all_to_all x1, waiting for transfers between devices, body(): grid = lax.all_to_all(grid, 'slab', split_axis=2, concat_axis=1, tiled=True)  26 us
    all_to_all x1, starting transfers between devices, body(): grid = lax.all_to_all(grid, 'slab', split_axis=2, concat_axis=1, tiled=True)  7.32 us
    dot_general x1, matrix products, along_z(): jnp.einsum('le,cije->cijl', matrix, grid, precision=lax.Precision.HIGHEST)  6.76 us
    unnamed x12, local copies, waits for them, and re-layouts  5.72 us
    dot_general x1, local copies, waits for them, and re-layouts, along_z(): jnp.einsum('le,cije->cijl', matrix, grid, precision=lax.Precision.HIGHEST)  4.44 us
    all_to_all x1, other arithmetic, body(): grid = lax.all_to_all(grid, 'slab', split_axis=2, concat_axis=1, tiled=True)  4.4 us
    dot_general x1, matrix products, along_x(): jnp.einsum('ia,cayz->ciyz', matrix, grid, precision=lax.Precision.HIGHEST)  3.79 us
    dot_general x1, matrix products, along_y(): jnp.einsum('jb,cibz->cijz', matrix, grid, precision=lax.Precision.HIGHEST)  2.95 us
  transfers between devices with their start and end apart: 1, of which 1 were waited for; matrix products, arithmetic and copies ran while one was open for 0% of the time, Pallas kernels for 0%

commit v1 on v0

--- a/solution.py
+++ b/solution.py
@@ -32,7 +32,10 @@
     matrix_y = band_matrix(offsets_y, coeffs_y, coarse_y, 0)
     matrix_z = band_matrix(offsets_z, coeffs_z, coarse_z, 0)
     grid = along_y(matrix_y, points)
-    grid = lax.all_to_all(grid, "slab", split_axis=2, concat_axis=1, tiled=True)
+    grid = jnp.concatenate(
+        lax.all_to_all(jnp.stack(jnp.split(grid, lax.axis_size("slab"), axis=2)), "slab", 0, 0),
+        axis=1,
+    )
     matrix_x = band_matrix(offsets_x, coeffs_x, grid.shape[1], 0)
     grid = along_x(matrix_x, grid)
     return along_z(matrix_z, grid)

time: 67.9 us -> 138 us (2.03); the launches traced: 67.6 us -> 136 us
  local copies, waits for them, and re-layouts: 14 us -> 82.8 us
    another operation x0 -> x35, local copies, waits for them, and re-layouts: none -> 59.6 us  [body(): jnp.stack(jnp.split(grid, lax.axis_size('slab'), axis=2))]
    unnamed x12 -> x61, local copies, waits for them, and re-layouts: 5.72 us -> 18 us
    transpose x1 -> x0, local copies, waits for them, and re-layouts: 2.29 us -> none  [along_y(): jnp.einsum('jb,cibz->cijz', matrix, grid, precision=lax.Precision.HIGHEST)]
where the time goes in v1:
time: 138 us; the launch traced here: 136 us
  local copies, waits for them, and re-layouts  82.8 us (60%)
  waiting for transfers between devices  25.9 us (19%)
  matrix products  12.5 us (9%)
  starting transfers between devices  7.5 us (5%)
  other arithmetic  6.6 us (5%)
    another operation x35, local copies, waits for them, and re-layouts, body(): jnp.stack(jnp.split(grid, lax.axis_size('slab'), axis=2))  59.6 us
    all_to_all x1, waiting for transfers between devices, body(): lax.all_to_all(jnp.stack(jnp.split(grid, lax.axis_size('slab'), axis=2)),...  25.9 us
    unnamed x61, local copies, waits for them, and re-layouts  18 us
    all_to_all x1, starting transfers between devices, body(): lax.all_to_all(jnp.stack(jnp.split(grid, lax.axis_size('slab'), axis=2)),...  7.5 us
    dot_general x1, matrix products, along_z(): jnp.einsum('le,cije->cijl', matrix, grid, precision=lax.Precision.HIGHEST)  6.76 us
    dot_general x1, local copies, waits for them, and re-layouts, along_z(): jnp.einsum('le,cije->cijl', matrix, grid, precision=lax.Precision.HIGHEST)  4.44 us
    all_to_all x1, other arithmetic, body(): lax.all_to_all(jnp.stack(jnp.split(grid, lax.axis_size('slab'), axis=2)),...  4.4 us
    dot_general x1, matrix products, along_x(): jnp.einsum('ia,cayz->ciyz', matrix, grid, precision=lax.Precision.HIGHEST)  3.79 us
  transfers between devices with their start and end apart: 1, of which 1 were waited for; matrix products, arithmetic and copies ran while one was open for 0% of the time, Pallas kernels for 0%

profile of v1, /device:TPU:0, one launch (start us, length us, event | category | flops | bytes accessed | tf_op | source)
XLA Modules:
  0.0 135.7 jit_solution(7784066049827033600)
XLA Ops:
  2.2 2.0 %convolution_bitcast_fusion = f32[4,4,256,64]{2,3,1,0:T(8,128)S(1)} fusion(f32[4,4,128,64]{2,3,1,0:T(8,128)S(1)} %copy-done, f32[256]{0:T(256)S(1)} %bitcast.106, s32[256]{0:T(256)S(1)} %get-tuple-element.53, f32[256]{0:T(256)S(1)} %bitcast.107, s32[256]{0:T(256)S(1)} %get-tuple-element.54, f32[256]{0:T(256)S(1)} %bitcast.108, ...), kind=kOutput, calls=%fused_computation.4 | convolution fusion | flops 403013632 | bytes 1581056 | tf_op jit(solution)/shard_map/jb,cibz->cijz/dot_general | solution.py:22
  4.1 3.9 %slice_bitcast_fusion.19 = (f32[1,4,4,8,64]{3,4,2,1,0:T(8,128)}, f32[1,4,4,8,64]{3,4,2,1,0:T(8,128)}, f32[1,4,4,8,64]{3,4,2,1,0:T(8,128)}, f32[1,4,4,8,64]{3,4,2...) fusion(f32[4,4,256,64]{2,3,1,0:T(8,128)S(1)} %convolution_bitca, ...), kind=kLoop, calls=%fused_computation.24 | loop fusion | bytes 851968 | tf_op jit(solution)/shard_map/stack | solution.py:36
  8.0 6.0 %slice_bitcast_fusion = (f32[1,4,4,8,64]{3,4,2,1,0:T(8,128)}, f32[1,4,4,8,64]{3,4,2,1,0:T(8,128)}, f32[1,4,4,8,64]{3,4,2,1,0:T(8,128)}, f32[1,4,4,8,64]{3,4,2,1,...) fusion(f32[4,4,256,64]{2,3,1,0:T(8,128)S(1)} %convolution_bitca, ...), kind=kLoop, calls=%fused_computation.5 | loop fusion | bytes 1245184 | tf_op jit(solution)/shard_map/stack | solution.py:36
  14.0 1.9 %copy.23 = f32[1,4,4,8,64]{4,3,2,1,0:T(8,128)} copy(f32[1,4,4,8,64]{3,4,2,1,0:T(8,128)} %get-tuple-element.24) | data formatting | bytes 65536 | tf_op jit(solution)/shard_map/stack | solution.py:36
  15.9 1.9 %copy.22 = f32[1,4,4,8,64]{4,3,2,1,0:T(8,128)} copy(f32[1,4,4,8,64]{3,4,2,1,0:T(8,128)} %get-tuple-element.25) | data formatting | bytes 65536 | tf_op jit(solution)/shard_map/stack | solution.py:36
  17.7 1.9 %copy.21 = f32[1,4,4,8,64]{4,3,2,1,0:T(8,128)} copy(f32[1,4,4,8,64]{3,4,2,1,0:T(8,128)} %get-tuple-element.26) | data formatting | bytes 65536 | tf_op jit(solution)/shard_map/stack | solution.py:36
  19.6 1.9 %copy.20 = f32[1,4,4,8,64]{4,3,2,1,0:T(8,128)} copy(f32[1,4,4,8,64]{3,4,2,1,0:T(8,128)} %get-tuple-element.27) | data formatting | bytes 65536 | tf_op jit(solution)/shard_map/stack | solution.py:36
  21.5 1.8 %copy.19 = f32[1,4,4,8,64]{4,3,2,1,0:T(8,128)} copy(f32[1,4,4,8,64]{3,4,2,1,0:T(8,128)} %get-tuple-element.28) | data formatting | bytes 65536 | tf_op jit(solution)/shard_map/stack | solution.py:36
  23.3 1.9 %copy.18 = f32[1,4,4,8,64]{4,3,2,1,0:T(8,128)} copy(f32[1,4,4,8,64]{3,4,2,1,0:T(8,128)} %get-tuple-element.29) | data formatting | bytes 65536 | tf_op jit(solution)/shard_map/stack | solution.py:36
  25.2 1.9 %copy.17 = f32[1,4,4,8,64]{4,3,2,1,0:T(8,128)} copy(f32[1,4,4,8,64]{3,4,2,1,0:T(8,128)} %get-tuple-element.30) | data formatting | bytes 65536 | tf_op jit(solution)/shard_map/stack | solution.py:36
  27.0 1.8 %copy.16 = f32[1,4,4,8,64]{4,3,2,1,0:T(8,128)} copy(f32[1,4,4,8,64]{3,4,2,1,0:T(8,128)} %get-tuple-element.31) | data formatting | bytes 65536 | tf_op jit(solution)/shard_map/stack | solution.py:36
  28.9 1.9 %copy.15 = f32[1,4,4,8,64]{4,3,2,1,0:T(8,128)} copy(f32[1,4,4,8,64]{3,4,2,1,0:T(8,128)} %get-tuple-element.32) | data formatting | bytes 65536 | tf_op jit(solution)/shard_map/stack | solution.py:36
  40.7 1.9 %copy.36 = f32[1,4,4,8,64]{4,3,2,1,0:T(8,128)} copy(f32[1,4,4,8,64]{3,4,2,1,0:T(8,128)} %get-tuple-element.11) | data formatting | bytes 65536 | tf_op jit(solution)/shard_map/stack | solution.py:36
  42.6 1.8 %copy.35 = f32[1,4,4,8,64]{4,3,2,1,0:T(8,128)} copy(f32[1,4,4,8,64]{3,4,2,1,0:T(8,128)} %get-tuple-element.12) | data formatting | bytes 65536 | tf_op jit(solution)/shard_map/stack | solution.py:36
  44.4 1.9 %copy.34 = f32[1,4,4,8,64]{4,3,2,1,0:T(8,128)} copy(f32[1,4,4,8,64]{3,4,2,1,0:T(8,128)} %get-tuple-element.13) | data formatting | bytes 65536 | tf_op jit(solution)/shard_map/stack | solution.py:36
  46.3 1.8 %copy.33 = f32[1,4,4,8,64]{4,3,2,1,0:T(8,128)} copy(f32[1,4,4,8,64]{3,4,2,1,0:T(8,128)} %get-tuple-element.14) | data formatting | bytes 65536 | tf_op jit(solution)/shard_map/stack | solution.py:36
  48.1 1.9 %copy.32 = f32[1,4,4,8,64]{4,3,2,1,0:T(8,128)} copy(f32[1,4,4,8,64]{3,4,2,1,0:T(8,128)} %get-tuple-element.15) | data formatting | bytes 65536 | tf_op jit(solution)/shard_map/stack | solution.py:36
  50.0 1.8 %copy.31 = f32[1,4,4,8,64]{4,3,2,1,0:T(8,128)} copy(f32[1,4,4,8,64]{3,4,2,1,0:T(8,128)} %get-tuple-element.16) | data formatting | bytes 65536 | tf_op jit(solution)/shard_map/stack | solution.py:36
  51.8 1.9 %copy.30 = f32[1,4,4,8,64]{4,3,2,1,0:T(8,128)} copy(f32[1,4,4,8,64]{3,4,2,1,0:T(8,128)} %get-tuple-element.17) | data formatting | bytes 65536 | tf_op jit(solution)/shard_map/stack | solution.py:36
  53.7 1.8 %copy.29 = f32[1,4,4,8,64]{4,3,2,1,0:T(8,128)} copy(f32[1,4,4,8,64]{3,4,2,1,0:T(8,128)} %get-tuple-element.18) | data formatting | bytes 65536 | tf_op jit(solution)/shard_map/stack | solution.py:36
  55.5 1.8 %copy.28 = f32[1,4,4,8,64]{4,3,2,1,0:T(8,128)} copy(f32[1,4,4,8,64]{3,4,2,1,0:T(8,128)} %get-tuple-element.19) | data formatting | bytes 65536 | tf_op jit(solution)/shard_map/stack | solution.py:36
  57.4 1.9 %copy.27 = f32[1,4,4,8,64]{4,3,2,1,0:T(8,128)} copy(f32[1,4,4,8,64]{3,4,2,1,0:T(8,128)} %get-tuple-element.20) | data formatting | bytes 65536 | tf_op jit(solution)/shard_map/stack | solution.py:36
  59.2 1.9 %copy.26 = f32[1,4,4,8,64]{4,3,2,1,0:T(8,128)} copy(f32[1,4,4,8,64]{3,4,2,1,0:T(8,128)} %get-tuple-element.21) | data formatting | bytes 65536 | tf_op jit(solution)/shard_map/stack | solution.py:36
  61.1 1.9 %copy.25 = f32[1,4,4,8,64]{4,3,2,1,0:T(8,128)} copy(f32[1,4,4,8,64]{3,4,2,1,0:T(8,128)} %get-tuple-element.22) | data formatting | bytes 65536 | tf_op jit(solution)/shard_map/stack | solution.py:36
  77.8 2.3 %reshape.47 = f32[32,1,8192]{2,1,0:T(1,128)} reshape(f32[32,4,4,8,64]{4,3,2,1,0:T(8,128)S(1)} %constant_dynamic-update-slice_fusion) | data formatting | bytes 2097152
  80.0 7.5 %all-to-all-start = ((f32[32,1,8192]{2,1,0:T(1,128)}), f32[32,1,8192]{2,1,0:T(1,128)S(1)}, u32[]{:S(2)}, u32[]{:S(2)}) async-start(f32[32,1,8192]{2,1,0:T(1,128)} %reshape.47), calls=%async_computation | async-start | bytes 2097152 | tf_op jit(solution)/shard_map/all_to_all | solution.py:36
  87.7 25.9 %all-to-all-done = f32[32,1,8192]{2,1,0:T(1,128)S(1)} async-done(((f32[32,1,8192]{2,1,0:T(1,128)}), f32[32,1,8192]{2,1,0:T(1,128)S(1)}, u32[]{:S(2)}, u32[]{:S(2)}) %all-to-all-start) | async-done | bytes 1048608 | tf_op jit(solution)/shard_map/all_to_all | solution.py:36
  114.1 4.4 %reduce = f32[32,8192]{1,0:T(8,128)} reduce(f32[32,1,8192]{2,1,0:T(1,128)S(1)} %all-to-all-done, f32[]{:T(128)} %broadcast.42), dimensions={1}, to_apply=%all_to_all.3.reduce_sub_computation | reduce | bytes 2097156 | tf_op jit(solution)/shard_map/all_to_all | solution.py:36
  118.5 2.0 %reshape.48 = f32[32,4,4,8,64]{4,3,2,1,0:T(8,128)S(1)} reshape(f32[32,8192]{1,0:T(8,128)} %reduce) | data formatting | bytes 2097152
  120.7 3.8 %fusion.2 = f32[4,8,64,256]{3,2,1,0:T(8,128)S(1)} fusion(f32[4,128,8,64]{3,2,1,0:T(8,128)S(1)} %bitcast.103, f32[256]{0:T(256)S(1)} %bitcast.110, s32[256]{0:T(256)S(1)} %get-tuple-element.50, f32[256]{0:T(256)S(1)} %bitcast.111, s32[256]{0:T(256)S(1)} %get-tuple-element.51, f32[256]{0:T(256)S(1)} %bitcast.112, s32[256]{0:T(256)S(1)} %get-tuple-element.49, ...), kind=kOutput, calls=%fused_computation.2 | convolution fusion | flops 805666816 | bytes 3153920 | tf_op jit(solution)/shard_map/ia,cayz->ciyz/dot_general | solution.py:18
  124.5 6.8 %fusion = f32[4,256,8,128]{3,1,2,0:T(8,128)S(1)} fusion(f32[4,8,64,256]{3,2,1,0:T(8,128)S(1)} %fusion.2, f32[128]{0:T(128)S(1)} %get-tuple-element.46, s32[128]{0:T(128)S(1)} %get-tuple-element.56, f32[128]{0:T(128)S(1)} %get-tuple-element.47, s32[128]{0:T(128)S(1)} %get-tuple-element.57, f32[128]{0:T(128)S(1)} %get-tuple-element.48, ...), kind=kOutput, calls=%fused_computation | convolution fusion | flops 805396480 | bytes 6295552 | tf_op jit(solution)/shard_map/le,cije->cijl/dot_general | solution.py:26
  131.3 4.4 %copy.45 = f32[4,256,8,128]{3,2,1,0:T(8,128)} copy(f32[4,256,8,128]{3,1,2,0:T(8,128)S(1)} %fusion) | data formatting | bytes 8388608 | tf_op jit(solution)/shard_map/le,cije->cijl/dot_general | solution.py:26
  (85 shorter events, 27.5 us)
Async XLA Ops:
  0.0 2.2 %copy-start = (f32[4,4,128,64]{2,3,1,0:T(8,128)S(1)}, f32[4,4,128,64]{2,3,1,0:T(8,128)}, u32[]{:S(2)}) copy-start(f32[4,4,128,64]{2,3,1,0:T(8,128)} %param.7) | copy-start | bytes 1572868
  63.7 13.7 %copy-start.9 = (f32[1,4,4,8,64]{4,3,2,1,0:T(8,128)S(1)}, f32[1,4,4,8,64]{4,3,2,1,0:T(8,128)}, u32[]{:S(2)}) copy-start(f32[1,4,4,8,64]{4,3,2,1,0:T(8,128)} %copy.28) | copy-start | bytes 98308
  63.7 13.7 %copy-start.8 = (f32[1,4,4,8,64]{4,3,2,1,0:T(8,128)S(1)}, f32[1,4,4,8,64]{4,3,2,1,0:T(8,128)}, u32[]{:S(2)}) copy-start(f32[1,4,4,8,64]{4,3,2,1,0:T(8,128)} %copy.29) | copy-start | bytes 98308
  63.7 13.7 %copy-start.7 = (f32[1,4,4,8,64]{4,3,2,1,0:T(8,128)S(1)}, f32[1,4,4,8,64]{4,3,2,1,0:T(8,128)}, u32[]{:S(2)}) copy-start(f32[1,4,4,8,64]{4,3,2,1,0:T(8,128)} %copy.30) | copy-start | bytes 98308
  63.7 13.7 %copy-start.6 = (f32[1,4,4,8,64]{4,3,2,1,0:T(8,128)S(1)}, f32[1,4,4,8,64]{4,3,2,1,0:T(8,128)}, u32[]{:S(2)}) copy-start(f32[1,4,4,8,64]{4,3,2,1,0:T(8,128)} %copy.31) | copy-start | bytes 98308
  63.7 13.7 %copy-start.5 = (f32[1,4,4,8,64]{4,3,2,1,0:T(8,128)S(1)}, f32[1,4,4,8,64]{4,3,2,1,0:T(8,128)}, u32[]{:S(2)}) copy-start(f32[1,4,4,8,64]{4,3,2,1,0:T(8,128)} %copy.32) | copy-start | bytes 98308
  63.8 13.8 %copy-start.4 = (f32[1,4,4,8,64]{4,3,2,1,0:T(8,128)S(1)}, f32[1,4,4,8,64]{4,3,2,1,0:T(8,128)}, u32[]{:S(2)}) copy-start(f32[1,4,4,8,64]{4,3,2,1,0:T(8,128)} %copy.33) | copy-start | bytes 98308
  63.8 13.8 %copy-start.3 = (f32[1,4,4,8,64]{4,3,2,1,0:T(8,128)S(1)}, f32[1,4,4,8,64]{4,3,2,1,0:T(8,128)}, u32[]{:S(2)}) copy-start(f32[1,4,4,8,64]{4,3,2,1,0:T(8,128)} %copy.34) | copy-start | bytes 98308
  63.8 13.8 %copy-start.2 = (f32[1,4,4,8,64]{4,3,2,1,0:T(8,128)S(1)}, f32[1,4,4,8,64]{4,3,2,1,0:T(8,128)}, u32[]{:S(2)}) copy-start(f32[1,4,4,8,64]{4,3,2,1,0:T(8,128)} %copy.35) | copy-start | bytes 98308
  63.8 13.8 %copy-start.1 = (f32[1,4,4,8,64]{4,3,2,1,0:T(8,128)S(1)}, f32[1,4,4,8,64]{4,3,2,1,0:T(8,128)}, u32[]{:S(2)}) copy-start(f32[1,4,4,8,64]{4,3,2,1,0:T(8,128)} %copy.36) | copy-start | bytes 98308
  77.7 9.8 %copy-start.11 = (f32[4,128]{1,0:T(4,128)S(1)}, f32[4,128]{1,0:T(4,128)}, u32[]{:S(2)}) copy-start(f32[4,128]{1,0:T(4,128)} %param.13) | copy-start | bytes 6148
  77.7 9.8 %copy-start.10 = (f32[4,256]{1,0:T(4,128)S(1)}, f32[4,256]{1,0:T(4,128)}, u32[]{:S(2)}) copy-start(f32[4,256]{1,0:T(4,128)} %param.9) | copy-start | bytes 12292
  77.7 9.9 %copy-start.13 = (s32[128]{0:T(128)S(1)}, s32[128]{0:T(128)}, u32[]{:S(2)}) copy-start(s32[128]{0:T(128)} %param.12) | copy-start | bytes 1540
  77.7 9.9 %copy-start.12 = (s32[256]{0:T(256)S(1)}, s32[256]{0:T(256)}, u32[]{:S(2)}) copy-start(s32[256]{0:T(256)} %param.8) | copy-start | bytes 3076
  80.0 33.5 %all-to-all-start = ((f32[32,1,8192]{2,1,0:T(1,128)}), f32[32,1,8192]{2,1,0:T(1,128)S(1)}, u32[]{:S(2)}, u32[]{:S(2)}) async-start(f32[32,1,8192]{2,1,0:T(1,128)} %reshape.47), calls=%async_computation | async-start | bytes 2097152 | tf_op jit(solution)/shard_map/all_to_all | solution.py:36
